TPU v7x, 32 devices: a whole 2x2x4 slice. The times are simulated.
32 devices in a mesh: rep: 4 (over x, y), dp: 8 (over z, core).
Axes of the slice: x: 2, y: 2, z: 4, core: 2. Of those that a mesh axis runs over, the one named last changes fastest.
Arguments:
- g_w_gate: bfloat16 [32, 2, 1024, 3072], P(('rep', 'dp')), parts along dimension 0
- g_w_up: bfloat16 [32, 2, 1024, 3072], P(('rep', 'dp')), parts along dimension 0
- g_w_down: bfloat16 [32, 2, 3072, 1024], P(('rep', 'dp')), parts along dimension 0
- w_gate: bfloat16 [2, 1024, 3072], replicated
- w_up: bfloat16 [2, 1024, 3072], replicated
- w_down: bfloat16 [2, 3072, 1024], replicated
- m_w_gate: float32 [2, 1024, 3072], P(None, 'dp')
- m_w_up: float32 [2, 1024, 3072], P(None, 'dp')
- m_w_down: float32 [2, 3072, 1024], P(None, 'dp')
- v_w_gate: float32 [2, 1024, 3072], P(None, 'dp')
- v_w_up: float32 [2, 1024, 3072], P(None, 'dp')
- v_w_down: float32 [2, 3072, 1024], P(None, 'dp')
Outputs:
- output 1: bfloat16 [8, 1024, 3072], P('rep'), parts along dimension 0
- output 2: bfloat16 [8, 1024, 3072], P('rep'), parts along dimension 0
- output 3: bfloat16 [8, 3072, 1024], P('rep'), parts along dimension 0
- output 4: float32 [8, 1024, 3072], P('rep', 'dp'), parts along dimension 0
- output 5: float32 [8, 1024, 3072], P('rep', 'dp'), parts along dimension 0
- output 6: float32 [8, 3072, 1024], P('rep', 'dp'), parts along dimension 0
- output 7: float32 [8, 1024, 3072], P('rep', 'dp'), parts along dimension 0
- output 8: float32 [8, 1024, 3072], P('rep', 'dp'), parts along dimension 0
- output 9: float32 [8, 3072, 1024], P('rep', 'dp'), parts along dimension 0
There are 4 independent parts. A program takes and returns all parts, laid end to end along the dimension named above; an argument that names none is the same for every part.
All inputs are finite; a program needn't handle non-finite values.
Results may differ from a plain program's by a relative error of at most 0.022.
Values are sent between devices in bfloat16 or wider.
A program may use at most 2 GiB of HBM per device.

v0:
```python
import jax
import jax.numpy as jnp
from jax import lax
from jax.sharding import PartitionSpec as P


def adamw(w, m, v, g):
    m = 0.9 * m + 0.1 * g
    v = 0.95 * v + 0.05 * g * g
    step = m * lax.rsqrt(v + 1e-8) + 0.1 * w
    return (w - 0.02 * step).astype(jnp.bfloat16), m, v


def solution(mesh):
    def step(*arrays):
        terms, weights, m, v = (arrays[i : i + 3] for i in (0, 3, 6, 9))
        gradients = [lax.psum_scatter(t[0], "dp", scatter_dimension=1, tiled=True).astype(jnp.float32) for t in terms]
        me = lax.axis_index("dp")
        own = [lax.dynamic_slice_in_dim(w, me * one.shape[1], one.shape[1], 1).astype(jnp.float32) for w, one in zip(weights, m, strict=True)]
        new = [adamw(w, m, v, g) for w, m, v, g in zip(own, m, v, gradients, strict=True)]
        whole = [lax.all_gather(one[0], "dp", axis=1, tiled=True) for one in new]
        return (*whole, *(one[1] for one in new), *(one[2] for one in new))

    all_of, cut = P(None, None, None), P(None, "dp", None)
    return jax.shard_map(
        step,
        mesh=mesh,
        in_specs=(P(("rep", "dp"), None, None, None),) * 3 + (all_of,) * 3 + (cut,) * 6,
        out_specs=(P("rep", None, None),) * 3 + (P("rep", "dp", None),) * 6,
        check_vma=False,
    )
```

profile of v0, /device:TPU:0, one launch (start us, length us, event | category | flops | bytes accessed | tf_op | source)
XLA Modules:
  0.0 786.1 jit_solution(16366913491548398811)
XLA Ops:
  7.2 0.0 reduce-scatter.8.cloned.1.call-start
  7.2 0.7 reduce-scatter.8.cloned.1.call-update
  7.9 0.0 reduce-scatter.6.cloned.1.call-start
  8.0 0.7 reduce-scatter.6.cloned.1.call-update
  8.7 0.0 reduce-scatter.4.cloned.1.call-start
  8.7 0.7 reduce-scatter.4.cloned.1.call-update
  9.4 0.0 all-gather.8.cloned.1.call-start
  9.4 132.6 %reduce-scatter.8.cloned.1.call-done = bf16[2,384,1024]{2,1,0:T(8,128)(2,1)} async-done(((bf16[2,3072,1024]{2,1,0:T(8,128)(2,1)}), bf16[2,384,1024]{2,1,0:T(8,128)(2,1)}) %reduce-scatter.8.cloned.1.call-update) | async-done | bytes 1572880 | tf_op jit(solution)/shard_map/reduce_scatter | solution.py:17
  142.0 7.1 fusion.10
  149.1 0.0 all-gather.6.cloned.1.call-start
  149.2 122.8 %reduce-scatter.6.cloned.1.call-done = bf16[2,128,3072]{2,1,0:T(8,128)(2,1)} async-done(((bf16[2,1024,3072]{2,1,0:T(8,128)(2,1)}), bf16[2,128,3072]{2,1,0:T(8,128)(2,1)}) %reduce-scatter.6.cloned.1.call-update) | async-done | bytes 1572880 | tf_op jit(solution)/shard_map/reduce_scatter | solution.py:17
  272.0 8.1 %fusion.6 = (bf16[2,128,3072]{2,1,0:T(8,128)(2,1)}, f32[2,128,3072]{2,1,0:T(8,128)}, f32[2,128,3072]{2,1,0:T(8,128)}) fusion(bf16[2,1024,3072]{2,1,0:T(8,128)(2,1)} %param.16, s32[]{:T(128)S(6)} %select_n.7, bf16[2,128,3072]{2,1,0:T(8,128)(2,1)} %reduce-scatter.6.cloned.1.call-done, f32[2,128,3072]{2,1,0:T(8,128)} %param.22, f32[2,128,3072]{2,1,0:T(8,128)} %param.19), kind=kLoop, calls=%fused_computation.18 | loop fusion | flops 12582912 | bytes 17301508 | tf_op jit(solution)/shard_map/convert_element_type | solution.py:11
  280.1 0.0 all-gather.4.cloned.1.call-start
  280.2 121.9 %reduce-scatter.4.cloned.1.call-done = bf16[2,128,3072]{2,1,0:T(8,128)(2,1)} async-done(((bf16[2,1024,3072]{2,1,0:T(8,128)(2,1)}), bf16[2,128,3072]{2,1,0:T(8,128)(2,1)}) %reduce-scatter.4.cloned.1.call-update) | async-done | bytes 1572880 | tf_op jit(solution)/shard_map/reduce_scatter | solution.py:17
  402.0 6.9 fusion.2
  409.0 0.0 all-gather.4.cloned.1.call-update
  409.0 110.1 %all-gather.8.cloned.1.call-done = bf16[2,3072,1024]{2,1,0:T(8,128)(2,1)} async-done(((bf16[2,384,1024]{2,1,0:T(8,128)(2,1)}), bf16[2,3072,1024]{2,1,0:T(8,128)(2,1)}) %all-gather.8.cloned.1.call-update) | async-done | bytes 12582928 | tf_op jit(solution)/shard_map/all_gather | solution.py:21
  519.1 117.1 %all-gather.6.cloned.1.call-done = bf16[2,1024,3072]{2,1,0:T(8,128)(2,1)} async-done(((bf16[2,128,3072]{2,1,0:T(8,128)(2,1)}), bf16[2,1024,3072]{2,1,0:T(8,128)(2,1)}) %all-gather.6.cloned.1.call-update) | async-done | bytes 12582928 | tf_op jit(solution)/shard_map/all_gather | solution.py:21
  636.2 117.1 %all-gather.4.cloned.1.call-done = bf16[2,1024,3072]{2,1,0:T(8,128)(2,1)} async-done(((bf16[2,128,3072]{2,1,0:T(8,128)(2,1)}), bf16[2,1024,3072]{2,1,0:T(8,128)(2,1)}) %all-gather.4.cloned.1.call-update) | async-done | bytes 12582928 | tf_op jit(solution)/shard_map/all_gather | solution.py:21
  753.3 12.4 %copy.24 = bf16[2,1024,3072]{2,1,0:T(8,128)(2,1)} copy(bf16[2,1024,3072]{2,1,0:T(8,128)(2,1)} %all-gather.4.cloned.1.call-done) | data formatting | bytes 25165824
  765.7 6.4 copy.25
  772.1 1.1 slice-done.1
  773.2 1.3 slice-done.2
  774.5 4.8 copy.26
  (13 shorter events, 0.1 us)
Async XLA Ops:
  7.2 134.8 %reduce-scatter.8.cloned.1.call-start = ((), (), s32[]{:S(2)}) async-start(), calls=%async_computation.7 | async-start | bytes 14155776 | tf_op jit(solution)/shard_map/reduce_scatter | solution.py:17
  7.9 264.1 %reduce-scatter.6.cloned.1.call-start = ((), (), s32[]{:S(2)}) async-start(), calls=%async_computation.5 | async-start | bytes 14155776 | tf_op jit(solution)/shard_map/reduce_scatter | solution.py:17
  8.7 393.4 %reduce-scatter.4.cloned.1.call-start = ((), (), s32[]{:S(2)}) async-start(), calls=%async_computation.3 | async-start | bytes 14155776 | tf_op jit(solution)/shard_map/reduce_scatter | solution.py:17
  8.7 133.3 %copy-start.1 = (f32[2,384,1024]{2,1,0:T(8,128)S(1)}, f32[2,384,1024]{2,1,0:T(8,128)}, u32[]{:S(2)}) copy-start(f32[2,384,1024]{2,1,0:T(8,128)} %param.23) | copy-start | bytes 9437188
  9.4 509.7 %all-gather.8.cloned.1.call-start = ((), (), s32[]{:S(2)}) async-start(), calls=%async_computation.8 | async-start | bytes 14155776 | tf_op jit(solution)/shard_map/all_gather | solution.py:21
  149.1 487.1 %all-gather.6.cloned.1.call-start = ((), (), s32[]{:S(2)}) async-start(), calls=%async_computation.6 | async-start | bytes 14155776 | tf_op jit(solution)/shard_map/all_gather | solution.py:21
  272.0 130.0 %copy-start.2 = (f32[2,128,3072]{2,1,0:T(8,128)S(1)}, f32[2,128,3072]{2,1,0:T(8,128)}, u32[]{:S(2)}) copy-start(f32[2,128,3072]{2,1,0:T(8,128)} %param.21) | copy-start | bytes 9437188
  280.1 473.2 %all-gather.4.cloned.1.call-start = ((), (), s32[]{:S(2)}) async-start(), calls=%async_computation.4 | async-start | bytes 14155776 | tf_op jit(solution)/shard_map/all_gather | solution.py:21
  753.3 12.4 %copy-start = (bf16[2,1024,3072]{2,1,0:T(8,128)(2,1)S(1)}, bf16[2,1024,3072]{2,1,0:T(8,128)(2,1)}, u32[]{:S(2)}) copy-start(bf16[2,1024,3072]{2,1,0:T(8,128)(2,1)} %all-gather.6.cloned.1.call-done) | copy-start | bytes 37748740
  753.3 18.8 %slice-start = ((s8[12582912]{0:T(1024)(128)(4,1)}), s8[4194304]{0:T(1024)(128)(4,1)S(1)}, s32[]{:S(2)}) async-start(s8[12582912]{0:T(1024)(128)(4,1)} %bitcast.6), calls=%async_computation.9 | async-start | bytes 8388608
  753.3 19.9 %slice-start.1 = ((s8[12582912]{0:T(1024)(128)(4,1)}), s8[4194304]{0:T(1024)(128)(4,1)S(1)}, s32[]{:S(2)}) async-start(s8[12582912]{0:T(1024)(128)(4,1)} %bitcast.6), calls=%async_computation.10 | async-start | bytes 8388608
  765.7 8.8 %slice-start.2 = ((s8[12582912]{0:T(1024)(128)(4,1)}), s8[4194304]{0:T(1024)(128)(4,1)S(1)}, s32[]{:S(2)}) async-start(s8[12582912]{0:T(1024)(128)(4,1)} %bitcast.6), calls=%async_computation.11 | async-start | bytes 8388608
Sparse Core Ops, SparseCore 0:
  10.3 131.6 reduce-scatter.7
  144.3 127.6 reduce-scatter.5
  274.3 127.6 reduce-scatter.3
  404.1 114.9 all-gather.7
  521.1 115.0 all-gather.5
  638.2 115.0 all-gather.3
where the time goes:
time: 786 us
  waiting for transfers between devices  724 us (92%)
  local copies, waits for them, and re-layouts  26 us (3%)
  other arithmetic  22.1 us (3%)
  between operations  14.1 us (2%)
    reduce_scatter x3, waiting for transfers between devices, step(): lax.psum_scatter(t[0], 'dp', scatter_dimension=1, tiled=True)  377 us
    all_gather x3, waiting for transfers between devices, step(): whole = [lax.all_gather(one[0], 'dp', axis=1, tiled=True) for one in new]  344 us
    unnamed x15, local copies, waits for them, and re-layouts  26 us
    convert_element_type x3, other arithmetic, adamw(): return ((w - 0.02 * step).astype(jnp.bfloat16), m, v)  22.1 us
  transfers between devices with their start and end apart: 6, of which 6 were waited for; matrix products, arithmetic and copies ran while one was open for 3% of the time, Pallas kernels for 0%

commit v1 on v0

v1 whole, which is shorter than its diff:
```python
import functools

import jax
import jax.numpy as jnp
from jax import lax
from jax.experimental import pallas as pl
from jax.experimental.pallas import tpu as pltpu
from jax.sharding import PartitionSpec as P

MESH = pl.DeviceIdType.MESH
CHIPS = 4
COLS = 1024
ROWS = 64
LAG = 1
AHEAD = 2
OWN = AHEAD + 3 * LAG + 1
SLOTS = 4
BAND = 16


def piece(j, per, r, cols):
    layer = j // (per // 2)
    k = j % (per // 2)
    across = cols // COLS
    return layer, pl.multiple_of((k // across) * ROWS, ROWS), pl.multiple_of((k % across) * COLS, COLS)


def kernel(steps, *refs):
    g, w, m, v, wo, mo, vo = (refs[i : i + 3] for i in range(0, 21, 3))
    (own, theirs, right, left, w_in, m_in, v_in, w_new, m_new, v_new,
     own_sem, theirs_send, theirs_recv, right_send, right_recv, left_send, left_recv,
     in_sem, mv_sem, new_sem, relay_right, relay_left, relay_core, gather_right, gather_left, gather_core) = refs[21:]
    per = steps // 3
    rep, me = lax.axis_index("rep"), lax.axis_index("dp")
    z, c = me // 2, me % 2
    last = CHIPS - 1
    partner, up, down = (rep, me + 1 - 2 * c), (rep, me + 2), (rep, me - 2)

    barrier = pltpu.get_barrier_semaphore()
    pl.semaphore_signal(barrier, inc=1, device_id=partner, device_id_type=MESH)

    @pl.when(z < last)
    def _():
        pl.semaphore_signal(barrier, inc=1, device_id=up, device_id_type=MESH)

    @pl.when(z > 0)
    def _():
        pl.semaphore_signal(barrier, inc=1, device_id=down, device_id_type=MESH)

    pl.semaphore_wait(barrier, 1 + jnp.minimum(z, 1) + jnp.minimum(last - z, 1))

    def remote(src, dst, send, recv, to):
        return pltpu.make_async_remote_copy(src_ref=src, dst_ref=dst, send_sem=send, recv_sem=recv, device_id=to, device_id_type=MESH)

    def each_weight(j, do):
        for k in range(3):

            @pl.when((j >= k * per) & (j < (k + 1) * per))
            def _(k=k):
                layer, row, col = piece(j - k * per, per, m[k].shape[1], m[k].shape[2])
                do(k, layer, pl.ds(row, ROWS), pl.ds(col, COLS))

    def load_terms(j):
        def do(k, layer, rows, cols):
            remote(g[k].at[layer, :, 1 - c, rows, cols], theirs.at[j], theirs_send, theirs_recv.at[j], partner).start()
            pltpu.make_async_copy(g[k].at[layer, :, c, rows, cols], own.at[j % OWN], own_sem.at[j % OWN]).start()

        each_weight(j, do)

    def load_state(j):
        s = j % SLOTS

        def do(k, layer, rows, cols):
            pltpu.make_async_copy(w[k].at[layer, z, c, rows, cols], w_in.at[s], in_sem.at[0, s]).start()
            pltpu.make_async_copy(m[k].at[layer, rows, cols], m_in.at[s], in_sem.at[1, s]).start()
            pltpu.make_async_copy(v[k].at[layer, rows, cols], v_in.at[s], in_sem.at[2, s]).start()

        each_weight(j, do)

    def bands(do):
        @pl.loop(0, ROWS // BAND)
        def _(t):
            do(pl.ds(pl.multiple_of(t * BAND, BAND), BAND))

    def forward(buf, slot, b, j, send, recv, to, first):
        @pl.when(first)
        def _():
            def do(r):
                total = own[j % OWN, b, r].astype(jnp.float32) + theirs[j, b, r].astype(jnp.float32)
                buf[slot, j, r] = total.astype(jnp.bfloat16)

            bands(do)

        @pl.when(jnp.logical_not(first))
        def _():
            remote(buf.at[slot, j], buf.at[slot, j], send.at[slot], recv.at[slot, j], to).wait_recv()

            def do(r):
                total = own[j % OWN, b, r].astype(jnp.float32) + theirs[j, b, r].astype(jnp.float32)
                buf[slot, j, r] = (total + buf[slot, j, r].astype(jnp.float32)).astype(jnp.bfloat16)

            bands(do)

        remote(buf.at[slot, j], buf.at[slot, j], send.at[slot], recv.at[slot, j], to).start()

    def new_copies(j, do):
        s = j % SLOTS

        def place(k, layer, rows, cols):
            dst = wo[k].at[layer, z, c, rows, cols]
            do(pltpu.make_async_copy(w_new.at[s], dst, new_sem.at[0, s]))
            do(remote(w_new.at[s], dst, new_sem.at[1, s], gather_core.at[k], partner))

            @pl.when(z < last)
            def _():
                do(remote(w_new.at[s], dst, new_sem.at[2, s], gather_right.at[jnp.minimum(z, 2), j], up))

            @pl.when(z > 0)
            def _():
                do(remote(w_new.at[s], dst, new_sem.at[3, s], gather_left.at[jnp.maximum(z, 1) - 1, j], down))

            do(pltpu.make_async_copy(m_new.at[s], mo[k].at[layer, rows, cols], mv_sem.at[0, s]))
            do(pltpu.make_async_copy(v_new.at[s], vo[k].at[layer, rows, cols], mv_sem.at[1, s]))

        each_weight(j, place)

    def wait_new(j):
        def do(copy):
            if copy.is_remote:
                copy.wait_send()
            else:
                copy.wait()

        new_copies(j, do)

    def step(j, with_right, with_left):
        s = j % SLOTS

        def do(r):
            total = own[j % OWN, z, r].astype(jnp.float32) + theirs[j, z, r].astype(jnp.float32)
            if with_right:
                total += right[jnp.maximum(z, 1) - 1, j, r].astype(jnp.float32)
            if with_left:
                total += left[jnp.minimum(z, 2), j, r].astype(jnp.float32)
            grad = total.astype(jnp.bfloat16).astype(jnp.float32)
            mean = 0.9 * m_in[s, r] + 0.1 * grad
            var = 0.95 * v_in[s, r] + 0.05 * grad * grad
            weight = w_in[s, r].astype(jnp.float32)
            change = mean * lax.rsqrt(var + 1e-8) + 0.1 * weight
            w_new[s, r] = (weight - 0.02 * change).astype(jnp.bfloat16)
            m_new[s, r] = mean
            v_new[s, r] = var

        bands(do)

    def final(j):
        s = j % SLOTS

        @pl.when(j >= SLOTS)
        def _():
            wait_new(j - SLOTS)

        pltpu.make_async_copy(w[0].at[0, 0, 0, pl.ds(0, ROWS), pl.ds(0, COLS)], w_in.at[s], in_sem.at[0, s]).wait()
        pltpu.make_async_copy(m[0].at[0, pl.ds(0, ROWS), pl.ds(0, COLS)], m_in.at[s], in_sem.at[1, s]).wait()
        pltpu.make_async_copy(v[0].at[0, pl.ds(0, ROWS), pl.ds(0, COLS)], v_in.at[s], in_sem.at[2, s]).wait()

        @pl.when(z > 0)
        def _():
            slot = jnp.maximum(z, 1) - 1
            remote(right.at[slot, j], right.at[slot, j], right_send.at[slot], right_recv.at[slot, j], down).wait_recv()

        @pl.when(z < last)
        def _():
            slot = jnp.minimum(z, 2)
            remote(left.at[slot, j], left.at[slot, j], left_send.at[slot], left_recv.at[slot, j], up).wait_recv()

        @pl.when(z == 0)
        def _():
            step(j, False, True)

        @pl.when(z == last)
        def _():
            step(j, True, False)

        @pl.when((z > 0) & (z < last))
        def _():
            step(j, True, True)

        new_copies(j, lambda copy: copy.start())

        @pl.when(j + 2 < steps)
        def _():
            load_state(j + 2)

    def relay(b, j, slot, recv, sent, to, more):
        def do(k, layer, rows, cols):
            here = wo[k].at[layer, b, c, rows, cols]
            remote(here, here, sent.at[slot], recv.at[slot, j], to).wait_recv()

            @pl.when(more)
            def _():
                remote(here, here, sent.at[slot], recv.at[slot, j], to).start()

            remote(here, here, relay_core, gather_core.at[k], partner).start()

        each_weight(j, do)

    done_at = [LAG * max(b, last - b) for b in range(CHIPS)]
    mine = LAG * jnp.maximum(z, last - z)

    for j in range(AHEAD):
        load_terms(j)
    for j in range(2):
        load_state(j)

    def within(j):
        return (j >= 0) & (j < steps)

    @pl.loop(0, steps + 2 * last * LAG)
    def _(i):
        @pl.when(i + AHEAD < steps)
        def _():
            load_terms(i + AHEAD)

        @pl.when(i < steps)
        def _():
            pltpu.make_async_copy(own.at[i % OWN], own.at[i % OWN], own_sem.at[i % OWN]).wait()
            remote(theirs.at[i], theirs.at[i], theirs_send, theirs_recv.at[i], partner).wait_recv()

        j_right = i - LAG * z
        j_left = i - LAG * (last - z)
        for n in range(last):
            b = last - n

            @pl.when(within(j_right) & (b > z))
            def _(b=b):
                forward(right, b - 1, b, j_right, right_send, right_recv, up, z == 0)

            @pl.when(within(j_left) & (n < z))
            def _(n=n):
                forward(left, n, n, j_left, left_send, left_recv, down, z == last)

        j_mine = i - mine

        @pl.when(within(j_mine))
        def _():
            final(j_mine)

        for n in range(last):
            b = last - n
            j = i - done_at[n] - LAG * (z - n)

            @pl.when(within(j) & (n < z))
            def _(n=n, j=j):
                relay(n, j, n, gather_right, relay_right, up, z < last)

            j = i - done_at[b] - LAG * (b - z)

            @pl.when(within(j) & (b > z))
            def _(b=b, j=j):
                relay(b, j, b - 1, gather_left, relay_left, down, z > 0)

    for j in range(steps - SLOTS, steps):
        wait_new(j)
    remote(theirs, theirs, theirs_send, theirs_recv.at[0], partner).wait_send()
    remote(right, right, relay_core, theirs_recv.at[0], partner).wait_send()
    for n in range(last):
        b = last - n

        @pl.when(b > z)
        def _(b=b):
            remote(right.at[0], right.at[0], right_send.at[b - 1], theirs_recv.at[0], up).wait_send()

        @pl.when(n < z)
        def _(n=n):
            remote(left.at[0], left.at[0], left_send.at[n], theirs_recv.at[0], down).wait_send()

        @pl.when((n < z) & (z < last))
        def _(n=n):
            remote(right.at[0], right.at[0], relay_right.at[n], theirs_recv.at[0], up).wait_send()

        @pl.when((b > z) & (z > 0))
        def _(b=b):
            remote(left.at[0], left.at[0], relay_left.at[b - 1], theirs_recv.at[0], down).wait_send()

    for k in range(3):
        arrived = wo[k].at[:, :, 1 - c]
        remote(arrived, arrived, theirs_send, gather_core.at[k], partner).wait_recv()


def solution(mesh):
    cores = mesh.shape["dp"] // CHIPS

    def step(*arrays):
        terms, weights, m, v = (arrays[i : i + 3] for i in (0, 3, 6, 9))
        steps = 3 * m[0].size // (ROWS * COLS)
        split = lambda a, one: a.reshape(one.shape[0], CHIPS, cores, *one.shape[1:])
        g = [split(a, one) for a, one in zip(terms, m, strict=True)]
        w = [split(a, one) for a, one in zip(weights, m, strict=True)]
        any_space = pl.BlockSpec(memory_space=pl.ANY)
        dma = pltpu.SemaphoreType.DMA
        half, full = jnp.bfloat16, jnp.float32
        outs = [jax.ShapeDtypeStruct(a.shape, a.dtype) for a in (*w, *m, *v)]
        got = pl.pallas_call(
            functools.partial(kernel, steps),
            out_shape=outs,
            in_specs=[any_space] * 12,
            out_specs=[any_space] * 9,
            scratch_shapes=[
                pltpu.VMEM((OWN, CHIPS, ROWS, COLS), half),
                pltpu.VMEM((steps, CHIPS, ROWS, COLS), half),
                pltpu.VMEM((CHIPS - 1, steps, ROWS, COLS), half),
                pltpu.VMEM((CHIPS - 1, steps, ROWS, COLS), half),
                pltpu.VMEM((SLOTS, ROWS, COLS), half),
                pltpu.VMEM((SLOTS, ROWS, COLS), full),
                pltpu.VMEM((SLOTS, ROWS, COLS), full),
                pltpu.VMEM((SLOTS, ROWS, COLS), half),
                pltpu.VMEM((SLOTS, ROWS, COLS), full),
                pltpu.VMEM((SLOTS, ROWS, COLS), full),
                dma((OWN,)),
                dma,
                dma((steps,)),
                dma((CHIPS - 1,)),
                dma((CHIPS - 1, steps)),
                dma((CHIPS - 1,)),
                dma((CHIPS - 1, steps)),
                dma((3, SLOTS)),
                dma((2, SLOTS)),
                dma((4, SLOTS)),
                dma((CHIPS - 1,)),
                dma((CHIPS - 1,)),
                dma,
                dma((CHIPS - 1, steps)),
                dma((CHIPS - 1, steps)),
                dma((3,)),
            ],
            compiler_params=pltpu.CompilerParams(collective_id=0, has_side_effects=True, vmem_limit_bytes=67_000_000),
            name="sum_step_gather",
        )(*g, *w, *m, *v)
        whole = [a.reshape(b.shape) for a, b in zip(got[:3], weights, strict=True)]
        return (*whole, *got[3:])

    all_of, cut = P(None, None, None), P(None, "dp", None)
    return jax.shard_map(
        step,
        mesh=mesh,
        in_specs=(P(("rep", "dp"), None, None, None),) * 3 + (all_of,) * 3 + (cut,) * 6,
        out_specs=(P("rep", None, None),) * 3 + (P("rep", "dp", None),) * 6,
        check_vma=False,
    )
```

time: 786 us -> 483 us (0.61)
  waiting for transfers between devices: 724 us -> 0 us
  Pallas kernels: 0 us -> 439 us
  other arithmetic: 22.1 us -> 0.01 us
  local copies, waits for them, and re-layouts: 26 us -> 43.3 us
  between operations: 14.1 us -> 0.69 us
    pallas_call x0 -> x1, Pallas kernels: none -> 439 us  [step(): pl.pallas_call(functools.partial(kernel, steps), out_shape=outs, in_specs...]
    reduce_scatter x3 -> x0, waiting for transfers between devices: 377 us -> none  [step(): lax.psum_scatter(t[0], 'dp', scatter_dimension=1, tiled=True)]
    all_gather x3 -> x0, waiting for transfers between devices: 344 us -> none  [step(): whole = [lax.all_gather(one[0], 'dp', axis=1, tiled=True) for one in new]]
    convert_element_type x3 -> x0, other arithmetic: 22.1 us -> none  [adamw(): return ((w - 0.02 * step).astype(jnp.bfloat16), m, v)]
    unnamed x15 -> x29, local copies, waits for them, and re-layouts: 26 us -> 43.3 us
  transfers between devices with their start and end apart: 6 -> 0, of which waited for: 6 -> 0; matrix products, arithmetic and copies ran while one was open for 3% -> 0% of each run, Pallas kernels for 0% -> 0%
where the time goes in v1:
time: 483 us
  Pallas kernels  439 us (91%)
  local copies, waits for them, and re-layouts  43.3 us (9%)
    pallas_call x1, Pallas kernels, step(): pl.pallas_call(functools.partial(kernel, steps), out_shape=outs, in_specs...  439 us
    unnamed x29, local copies, waits for them, and re-layouts  43.3 us

profile of v1, /device:TPU:0, one launch (start us, length us, event | category | flops | bytes accessed | tf_op | source)
XLA Modules:
  0.0 482.9 jit_solution(3633569722774989109)
XLA Ops:
  0.6 438.9 %sum_step_gather.1 = (bf16[2,4,2,128,3072]{4,3,2,1,0:T(8,128)(2,1)}, bf16[2,4,2,128,3072]{4,3,2,1,0:T(8,128)(2,1)}, bf16[2,4,2,384,1024]{4,3,2,1,0:T(8,128)(2,1)...) custom-call(bf16[2,4,2,128,3072]{4,3,2,1,0:T(8,128)(2,1)} %bitcast.1, ...), custom_call_target="tpu_custom_call" | custom-call | tf_op jit(solution)/shard_map/sum_step_gather/pallas_call | solution.py:304
  439.6 0.0 copy-start
  439.6 0.0 slice-start
  439.6 0.0 slice-start.1
  439.6 12.4 %copy.30 = bf16[2,1024,3072]{2,1,0:T(8,128)(2,1)} copy(bf16[2,1024,3072]{2,1,0:T(8,128)(2,1)} %bitcast.13) | data formatting | bytes 25165824
  452.0 0.0 copy-done
  452.0 0.0 slice-start.2
  452.1 6.4 %copy.31 = bf16[2,1024,3072]{2,1,0:T(8,128)(2,1)} copy(bf16[2,1024,3072]{2,1,0:T(8,128)(2,1)S(1)} %bitcast.12) | data formatting | bytes 25165824
  458.4 0.0 slice-done
  458.4 1.0 slice-done.1
  459.5 1.3 slice-done.2
  460.8 5.3 %copy.32 = bf16[2,3072,1024]{2,1,0:T(8,128)(2,1)} copy(bf16[2,3072,1024]{2,1,0:T(8,128)(2,1)S(1)} %bitcast.11) | data formatting | bytes 25165824
  466.1 0.0 copy-done.6
  466.1 1.7 copy.33
  467.8 1.4 copy-done.5
  469.1 1.7 copy.34
  470.8 1.4 copy-done.4
  472.1 1.7 copy.35
  473.8 1.4 copy-done.3
  475.2 1.7 copy.36
  476.8 1.4 copy-done.2
  478.2 1.7 copy.37
  479.9 1.4 copy-done.1
  481.2 1.7 copy.38
  (7 shorter events, 0.0 us)
Async XLA Ops:
  439.6 12.5 %copy-start = (bf16[2,4,2,128,3072]{4,3,2,1,0:T(8,128)(2,1)S(1)}, bf16[2,4,2,128,3072]{4,3,2,1,0:T(8,128)(2,1)}, u32[]{:S(2)}) copy-start(bf16[2,4,2,128,3072]{4,3,2,1,0:T(8,128)(2,1)} %get-tuple-element.19) | copy-start | bytes 37748740
  439.6 18.8 %slice-start = ((s8[12582912]{0:T(1024)(128)(4,1)}), s8[4194304]{0:T(1024)(128)(4,1)S(1)}, s32[]{:S(2)}) async-start(s8[12582912]{0:T(1024)(128)(4,1)} %bitcast.9), calls=%async_computation | async-start | bytes 8388608
  439.6 19.9 %slice-start.1 = ((s8[12582912]{0:T(1024)(128)(4,1)}), s8[4194304]{0:T(1024)(128)(4,1)S(1)}, s32[]{:S(2)}) async-start(s8[12582912]{0:T(1024)(128)(4,1)} %bitcast.9), calls=%async_computation.1 | async-start | bytes 8388608
  452.0 8.7 %slice-start.2 = ((s8[12582912]{0:T(1024)(128)(4,1)}), s8[4194304]{0:T(1024)(128)(4,1)S(1)}, s32[]{:S(2)}) async-start(s8[12582912]{0:T(1024)(128)(4,1)} %bitcast.9), calls=%async_computation.2 | async-start | bytes 8388608
  460.8 5.3 %copy-start.6 = (f32[2,128,3072]{2,1,0:T(8,128)S(1)}, f32[2,128,3072]{2,1,0:T(8,128)}, u32[]{:S(2)}) copy-start(f32[2,128,3072]{2,1,0:T(8,128)} %get-tuple-element.39) | copy-start | bytes 9437188
  466.1 3.0 copy-start.5
  469.1 3.0 copy-start.4
  472.1 3.0 copy-start.3
  475.2 3.0 copy-start.2
  478.2 3.0 copy-start.1

commit v2 on v1

--- a/solution.py
+++ b/solution.py
@@ -10,11 +10,13 @@
 MESH = pl.DeviceIdType.MESH
 CHIPS = 4
 COLS = 1024
-ROWS = 64
+ROWS = 32
 LAG = 1
 AHEAD = 2
 OWN = AHEAD + 3 * LAG + 1
 SLOTS = 4
+THEIRS = OWN + 2
+CHUNKS = 8
 BAND = 16
 
 
@@ -26,10 +28,10 @@
 
 
 def kernel(steps, *refs):
-    g, w, m, v, wo, mo, vo = (refs[i : i + 3] for i in range(0, 21, 3))
-    (own, theirs, right, left, w_in, m_in, v_in, w_new, m_new, v_new,
-     own_sem, theirs_send, theirs_recv, right_send, right_recv, left_send, left_recv,
-     in_sem, mv_sem, new_sem, relay_right, relay_left, relay_core, gather_right, gather_left, gather_core) = refs[21:]
+    g, w, m, v, wo = (refs[i : i + 3] for i in range(0, 15, 3))
+    (m_new, v_new, own, theirs, right, left, w_in, m_in, v_in, w_new,
+     own_sem, theirs_send, theirs_recv, theirs_free, right_send, right_recv, left_send, left_recv,
+     in_sem, new_sem, relay_right, relay_left, relay_core, gather_right, gather_left, gather_core) = refs[15:]
     per = steps // 3
     rep, me = lax.axis_index("rep"), lax.axis_index("dp")
     z, c = me // 2, me % 2
@@ -61,8 +63,14 @@
                 do(k, layer, pl.ds(row, ROWS), pl.ds(col, COLS))
 
     def load_terms(j):
+        t = j % THEIRS
+
+        @pl.when(j >= THEIRS)
+        def _():
+            pl.semaphore_wait(theirs_free, 1)
+
         def do(k, layer, rows, cols):
-            remote(g[k].at[layer, :, 1 - c, rows, cols], theirs.at[j], theirs_send, theirs_recv.at[j], partner).start()
+            remote(g[k].at[layer, :, 1 - c, rows, cols], theirs.at[t], theirs_send, theirs_recv.at[t], partner).start()
             pltpu.make_async_copy(g[k].at[layer, :, c, rows, cols], own.at[j % OWN], own_sem.at[j % OWN]).start()
 
         each_weight(j, do)
@@ -86,7 +94,7 @@
         @pl.when(first)
         def _():
             def do(r):
-                total = own[j % OWN, b, r].astype(jnp.float32) + theirs[j, b, r].astype(jnp.float32)
+                total = own[j % OWN, b, r].astype(jnp.float32) + theirs[j % THEIRS, b, r].astype(jnp.float32)
                 buf[slot, j, r] = total.astype(jnp.bfloat16)
 
             bands(do)
@@ -96,7 +104,7 @@
             remote(buf.at[slot, j], buf.at[slot, j], send.at[slot], recv.at[slot, j], to).wait_recv()
 
             def do(r):
-                total = own[j % OWN, b, r].astype(jnp.float32) + theirs[j, b, r].astype(jnp.float32)
+                total = own[j % OWN, b, r].astype(jnp.float32) + theirs[j % THEIRS, b, r].astype(jnp.float32)
                 buf[slot, j, r] = (total + buf[slot, j, r].astype(jnp.float32)).astype(jnp.bfloat16)
 
             bands(do)
@@ -118,9 +126,6 @@
             @pl.when(z > 0)
             def _():
                 do(remote(w_new.at[s], dst, new_sem.at[3, s], gather_left.at[jnp.maximum(z, 1) - 1, j], down))
-
-            do(pltpu.make_async_copy(m_new.at[s], mo[k].at[layer, rows, cols], mv_sem.at[0, s]))
-            do(pltpu.make_async_copy(v_new.at[s], vo[k].at[layer, rows, cols], mv_sem.at[1, s]))
 
         each_weight(j, place)
 
@@ -137,7 +142,7 @@
         s = j % SLOTS
 
         def do(r):
-            total = own[j % OWN, z, r].astype(jnp.float32) + theirs[j, z, r].astype(jnp.float32)
+            total = own[j % OWN, z, r].astype(jnp.float32) + theirs[j % THEIRS, z, r].astype(jnp.float32)
             if with_right:
                 total += right[jnp.maximum(z, 1) - 1, j, r].astype(jnp.float32)
             if with_left:
@@ -148,8 +153,8 @@
             weight = w_in[s, r].astype(jnp.float32)
             change = mean * lax.rsqrt(var + 1e-8) + 0.1 * weight
             w_new[s, r] = (weight - 0.02 * change).astype(jnp.bfloat16)
-            m_new[s, r] = mean
-            v_new[s, r] = var
+            m_new[j, r] = mean
+            v_new[j, r] = var
 
         bands(do)
 
@@ -225,7 +230,8 @@
         @pl.when(i < steps)
         def _():
             pltpu.make_async_copy(own.at[i % OWN], own.at[i % OWN], own_sem.at[i % OWN]).wait()
-            remote(theirs.at[i], theirs.at[i], theirs_send, theirs_recv.at[i], partner).wait_recv()
+            t = i % THEIRS
+            remote(theirs.at[t], theirs.at[t], theirs_send, theirs_recv.at[t], partner).wait_recv()
 
         j_right = i - LAG * z
         j_left = i - LAG * (last - z)
@@ -246,6 +252,12 @@
         def _():
             final(j_mine)
 
+        j_free = i - last * LAG
+
+        @pl.when((j_free >= 0) & (j_free < steps - THEIRS))
+        def _():
+            pl.semaphore_signal(theirs_free, inc=1, device_id=partner, device_id_type=MESH)
+
         for n in range(last):
             b = last - n
             j = i - done_at[n] - LAG * (z - n)
@@ -262,7 +274,9 @@
 
     for j in range(steps - SLOTS, steps):
         wait_new(j)
-    remote(theirs, theirs, theirs_send, theirs_recv.at[0], partner).wait_send()
+    for k in range(3):
+        sent = g[k].at[:, :, 1 - c]
+        remote(sent, sent, theirs_send, theirs_recv.at[0], partner).wait_send()
     remote(right, right, relay_core, theirs_recv.at[0], partner).wait_send()
     for n in range(last):
         b = last - n
@@ -286,6 +300,44 @@
     for k in range(3):
         arrived = wo[k].at[:, :, 1 - c]
         remote(arrived, arrived, theirs_send, gather_core.at[k], partner).wait_recv()
+
+
+def finish(steps, *refs):
+    w, m, v = refs[:3], refs[3], refs[4]
+    wo, mo, vo = (refs[i : i + 3] for i in range(5, 14, 3))
+    stage, in_sem, out_sem, m_sem, v_sem = refs[14], refs[15], refs[16], refs[17], refs[18]
+    per = steps // 3
+    height = [a.shape[1] // (CHUNKS // 2) for a in w]
+
+    def part(a, k, n):
+        return a[k].at[n // (CHUNKS // 2), pl.ds(n % (CHUNKS // 2) * height[k], height[k])]
+
+    def held(k, n):
+        return stage[k].at[n]
+
+    for n in range(CHUNKS):
+        for k in range(3):
+            pltpu.make_async_copy(part(w, k, n), held(k, n), in_sem.at[k, n]).start()
+
+    for k in range(3):
+
+        @pl.loop(0, per)
+        def _(j, k=k):
+            layer, row, col = piece(j, per, mo[k].shape[1], mo[k].shape[2])
+            place = (layer, pl.ds(row, ROWS), pl.ds(col, COLS))
+            pltpu.make_async_copy(m.at[k * per + j], mo[k].at[place], m_sem).start()
+            pltpu.make_async_copy(v.at[k * per + j], vo[k].at[place], v_sem).start()
+
+    for n in range(CHUNKS):
+        for k in range(3):
+            pltpu.make_async_copy(part(w, k, n), held(k, n), in_sem.at[k, n]).wait()
+            pltpu.make_async_copy(held(k, n), part(wo, k, n), out_sem.at[k, n]).start()
+
+    for n in range(CHUNKS):
+        for k in range(3):
+            pltpu.make_async_copy(held(k, n), part(wo, k, n), out_sem.at[k, n]).wait()
+    pltpu.make_async_copy(m, m, m_sem).wait()
+    pltpu.make_async_copy(v, v, v_sem).wait()
 
 
 def solution(mesh):
@@ -297,35 +349,33 @@
         split = lambda a, one: a.reshape(one.shape[0], CHIPS, cores, *one.shape[1:])
         g = [split(a, one) for a, one in zip(terms, m, strict=True)]
         w = [split(a, one) for a, one in zip(weights, m, strict=True)]
-        any_space = pl.BlockSpec(memory_space=pl.ANY)
+        any_space, hbm, vmem = (pl.BlockSpec(memory_space=a) for a in (pl.ANY, pltpu.HBM, pltpu.VMEM))
         dma = pltpu.SemaphoreType.DMA
         half, full = jnp.bfloat16, jnp.float32
-        outs = [jax.ShapeDtypeStruct(a.shape, a.dtype) for a in (*w, *m, *v)]
+        state = (steps, ROWS, COLS)
         got = pl.pallas_call(
             functools.partial(kernel, steps),
-            out_shape=outs,
+            out_shape=[*(pltpu.HBM(a.shape, a.dtype) for a in w), pltpu.VMEM(state, full), pltpu.VMEM(state, full)],
             in_specs=[any_space] * 12,
-            out_specs=[any_space] * 9,
+            out_specs=[hbm] * 3 + [vmem] * 2,
             scratch_shapes=[
                 pltpu.VMEM((OWN, CHIPS, ROWS, COLS), half),
-                pltpu.VMEM((steps, CHIPS, ROWS, COLS), half),
+                pltpu.VMEM((THEIRS, CHIPS, ROWS, COLS), half),
                 pltpu.VMEM((CHIPS - 1, steps, ROWS, COLS), half),
                 pltpu.VMEM((CHIPS - 1, steps, ROWS, COLS), half),
                 pltpu.VMEM((SLOTS, ROWS, COLS), half),
                 pltpu.VMEM((SLOTS, ROWS, COLS), full),
                 pltpu.VMEM((SLOTS, ROWS, COLS), full),
                 pltpu.VMEM((SLOTS, ROWS, COLS), half),
-                pltpu.VMEM((SLOTS, ROWS, COLS), full),
-                pltpu.VMEM((SLOTS, ROWS, COLS), full),
                 dma((OWN,)),
                 dma,
-                dma((steps,)),
+                dma((THEIRS,)),
+                pltpu.SemaphoreType.REGULAR,
                 dma((CHIPS - 1,)),
                 dma((CHIPS - 1, steps)),
                 dma((CHIPS - 1,)),
                 dma((CHIPS - 1, steps)),
                 dma((3, SLOTS)),
-                dma((2, SLOTS)),
                 dma((4, SLOTS)),
                 dma((CHIPS - 1,)),
                 dma((CHIPS - 1,)),
@@ -334,11 +384,21 @@
                 dma((CHIPS - 1, steps)),
                 dma((3,)),
             ],
-            compiler_params=pltpu.CompilerParams(collective_id=0, has_side_effects=True, vmem_limit_bytes=67_000_000),
+            compiler_params=pltpu.CompilerParams(collective_id=0, has_side_effects=True, vmem_limit_bytes=46_000_000),
             name="sum_step_gather",
         )(*g, *w, *m, *v)
-        whole = [a.reshape(b.shape) for a, b in zip(got[:3], weights, strict=True)]
-        return (*whole, *got[3:])
+        new = [pltpu.with_memory_space_constraint(a.reshape(b.shape), pltpu.HBM) for a, b in zip(got[:3], weights, strict=True)]
+        mv = [pltpu.with_memory_space_constraint(a, pltpu.VMEM) for a in got[3:]]
+        stage = [pltpu.VMEM((CHUNKS, a.shape[1] // (CHUNKS // 2), a.shape[2]), half) for a in weights]
+        return pl.pallas_call(
+            functools.partial(finish, steps),
+            out_shape=[pltpu.HBM(a.shape, a.dtype) for a in (*weights, *m, *v)],
+            in_specs=[hbm] * 3 + [vmem] * 2,
+            out_specs=[hbm] * 9,
+            scratch_shapes=[stage, dma((3, CHUNKS)), dma((3, CHUNKS)), dma, dma],
+            compiler_params=pltpu.CompilerParams(vmem_limit_bytes=46_000_000),
+            name="finish",
+        )(*new, *mv)
 
     all_of, cut = P(None, None, None), P(None, "dp", None)
     return jax.shard_map(

time: 483 us -> 464 us (0.961)
  local copies, waits for them, and re-layouts: 43.3 us -> 0 us
  Pallas kernels: 439 us -> 463 us
    unnamed x29 -> x0, local copies, waits for them, and re-layouts: 43.3 us -> none
    pallas_call x1 -> x2, Pallas kernels: 439 us -> 463 us  [the longest x1 432 us: step(): pl.pallas_call(functools.partial(kernel, steps), out_shape=[*(pltpu.HBM(a...]
where the time goes in v2:
time: 464 us
  Pallas kernels  463 us (100%)
    pallas_call x1, Pallas kernels, step(): pl.pallas_call(functools.partial(kernel, steps), out_shape=[*(pltpu.HBM(a...  432 us
    pallas_call x1, Pallas kernels, step(): pl.pallas_call(functools.partial(finish, steps), out_shape=[pltpu.HBM(a.s...  31.3 us

profile of v2, /device:TPU:0, one launch (start us, length us, event | category | flops | bytes accessed | tf_op | source)
XLA Modules:
  0.0 464.1 jit_solution(7132609610517675791)
XLA Ops:
  0.6 432.1 %sum_step_gather.1 = (bf16[2,4,2,128,3072]{4,3,2,1,0:T(8,128)(2,1)}, bf16[2,4,2,128,3072]{4,3,2,1,0:T(8,128)(2,1)}, bf16[2,4,2,384,1024]{4,3,2,1,0:T(8,128)(2,1)...) custom-call(bf16[2,4,2,128,3072]{4,3,2,1,0:T(8,128)(2,1)} %bitcast.12, bf16[2,4,2,128,3072]{4,3,2,1,0:T(8,128)(2,1)} %bitcast.13, ...), custom_call_target="tpu_custom_call" | custom-call | tf_op jit(solution)/shard_map/sum_step_gather/pallas_call | solution.py:356
  432.8 31.3 %finish.1 = (bf16[2,1024,3072]{2,1,0:T(8,128)(2,1)}, bf16[2,1024,3072]{2,1,0:T(8,128)(2,1)}, bf16[2,3072,1024]{2,1,0:T(8,128)(2,1)}, f32[2,128,3072]{2,1,0:T(8,1...) custom-call(bf16[2,1024,3072]{2,1,0:T(8,128)(2,1)} %bitcast.9, ...), custom_call_target="tpu_custom_call" | custom-call | tf_op jit(solution)/shard_map/finish/pallas_call | solution.py:393

commit v3 on v2

v3 whole, which is shorter than its diff:
```python
import functools

import jax
import jax.numpy as jnp
from jax import lax
from jax.experimental import pallas as pl
from jax.experimental.pallas import tpu as pltpu
from jax.sharding import PartitionSpec as P

MESH = pl.DeviceIdType.MESH
CHIPS = 4
COLS = 1024
ROWS = 32
LAG = 1
AHEAD = 2
OWN = AHEAD + 3 * LAG + 1
SLOTS = 4
THEIRS = OWN + 2
RING = 8
GRANT = 9_400_000
BAND = 16


def piece(j, per, r, cols):
    layer = j // (per // 2)
    k = j % (per // 2)
    across = cols // COLS
    return layer, pl.multiple_of((k // across) * ROWS, ROWS), pl.multiple_of((k % across) * COLS, COLS)


def kernel(steps, *refs):
    g, w, m, v, wo = (refs[i : i + 3] for i in range(0, 15, 3))
    (m_new, v_new, own, theirs, right, left, w_in, m_in, v_in,
     own_sem, theirs_send, theirs_recv, theirs_free, right_send, right_recv, right_free, left_send, left_recv, left_free,
     in_sem, new_sem, relay_right, relay_left, relay_core, gather_right, gather_left, gather_core) = refs[15:]
    per = steps // 3
    rep, me = lax.axis_index("rep"), lax.axis_index("dp")
    z, c = me // 2, me % 2
    last = CHIPS - 1
    partner, up, down = (rep, me + 1 - 2 * c), (rep, me + 2), (rep, me - 2)

    barrier = pltpu.get_barrier_semaphore()
    pl.semaphore_signal(barrier, inc=1, device_id=partner, device_id_type=MESH)

    @pl.when(z < last)
    def _():
        pl.semaphore_signal(barrier, inc=1, device_id=up, device_id_type=MESH)

    @pl.when(z > 0)
    def _():
        pl.semaphore_signal(barrier, inc=1, device_id=down, device_id_type=MESH)

    pl.semaphore_wait(barrier, 1 + jnp.minimum(z, 1) + jnp.minimum(last - z, 1))

    def remote(src, dst, send, recv, to):
        return pltpu.make_async_remote_copy(src_ref=src, dst_ref=dst, send_sem=send, recv_sem=recv, device_id=to, device_id_type=MESH)

    def each_weight(j, do):
        for k in range(3):

            @pl.when((j >= k * per) & (j < (k + 1) * per))
            def _(k=k):
                layer, row, col = piece(j - k * per, per, m[k].shape[1], m[k].shape[2])
                do(k, layer, pl.ds(row, ROWS), pl.ds(col, COLS))

    def load_terms(j):
        t = j % THEIRS

        @pl.when(j >= THEIRS)
        def _():
            pl.semaphore_wait(theirs_free, 1)

        def do(k, layer, rows, cols):
            remote(g[k].at[layer, :, 1 - c, rows, cols], theirs.at[t], theirs_send, theirs_recv.at[t], partner).start()
            pltpu.make_async_copy(g[k].at[layer, :, c, rows, cols], own.at[j % OWN], own_sem.at[j % OWN]).start()

        each_weight(j, do)

    def load_state(j):
        s = j % SLOTS

        def do(k, layer, rows, cols):
            pltpu.make_async_copy(w[k].at[layer, z, c, rows, cols], w_in.at[s], in_sem.at[0, s]).start()
            pltpu.make_async_copy(m[k].at[layer, rows, cols], m_in.at[s], in_sem.at[1, s]).start()
            pltpu.make_async_copy(v[k].at[layer, rows, cols], v_in.at[s], in_sem.at[2, s]).start()

        each_weight(j, do)

    def bands(do):
        @pl.loop(0, ROWS // BAND)
        def _(t):
            do(pl.ds(pl.multiple_of(t * BAND, BAND), BAND))

    def forward(buf, slot, b, j, send, recv, to, first):
        q = j % RING

        @pl.when(first)
        def _():
            def do(r):
                total = own[j % OWN, b, r].astype(jnp.float32) + theirs[j % THEIRS, b, r].astype(jnp.float32)
                buf[slot, q, r] = total.astype(jnp.bfloat16)

            bands(do)

        @pl.when(jnp.logical_not(first))
        def _():
            remote(buf.at[slot, q], buf.at[slot, q], send.at[slot, q], recv.at[slot, q], to).wait_recv()

            def do(r):
                total = own[j % OWN, b, r].astype(jnp.float32) + theirs[j % THEIRS, b, r].astype(jnp.float32)
                buf[slot, q, r] = (total + buf[slot, q, r].astype(jnp.float32)).astype(jnp.bfloat16)

            bands(do)

        remote(buf.at[slot, q], buf.at[slot, q], send.at[slot, q], recv.at[slot, q], to).start()

    def step(j, k, layer, rows, cols, with_right, with_left):
        s, q = j % SLOTS, j % RING

        def do(r):
            total = own[j % OWN, z, r].astype(jnp.float32) + theirs[j % THEIRS, z, r].astype(jnp.float32)
            if with_right:
                total += right[jnp.maximum(z, 1) - 1, q, r].astype(jnp.float32)
            if with_left:
                total += left[jnp.minimum(z, 2), q, r].astype(jnp.float32)
            grad = total.astype(jnp.bfloat16).astype(jnp.float32)
            mean = 0.9 * m_in[s, r] + 0.1 * grad
            var = 0.95 * v_in[s, r] + 0.05 * grad * grad
            weight = w_in[s, r].astype(jnp.float32)
            change = mean * lax.rsqrt(var + 1e-8) + 0.1 * weight
            place = pl.ds(pl.multiple_of(rows.start + r.start, BAND), BAND)
            wo[k][layer, z, c, place, cols] = (weight - 0.02 * change).astype(jnp.bfloat16)
            m_new[j, r] = mean
            v_new[j, r] = var

        bands(do)

    def final(j):
        s, q = j % SLOTS, j % RING
        pltpu.make_async_copy(w[0].at[0, 0, 0, pl.ds(0, ROWS), pl.ds(0, COLS)], w_in.at[s], in_sem.at[0, s]).wait()
        pltpu.make_async_copy(m[0].at[0, pl.ds(0, ROWS), pl.ds(0, COLS)], m_in.at[s], in_sem.at[1, s]).wait()
        pltpu.make_async_copy(v[0].at[0, pl.ds(0, ROWS), pl.ds(0, COLS)], v_in.at[s], in_sem.at[2, s]).wait()

        @pl.when(z > 0)
        def _():
            slot = jnp.maximum(z, 1) - 1
            remote(right.at[slot, q], right.at[slot, q], right_send.at[slot, q], right_recv.at[slot, q], down).wait_recv()

        @pl.when(z < last)
        def _():
            slot = jnp.minimum(z, 2)
            remote(left.at[slot, q], left.at[slot, q], left_send.at[slot, q], left_recv.at[slot, q], up).wait_recv()

        def do(k, layer, rows, cols):
            @pl.when(z == 0)
            def _():
                step(j, k, layer, rows, cols, False, True)

            @pl.when(z == last)
            def _():
                step(j, k, layer, rows, cols, True, False)

            @pl.when((z > 0) & (z < last))
            def _():
                step(j, k, layer, rows, cols, True, True)

            here = wo[k].at[layer, z, c, rows, cols]

            @pl.when(z < last)
            def _():
                remote(here, here, new_sem.at[0], gather_right.at[jnp.minimum(z, 2), j], up).start()

            @pl.when(z > 0)
            def _():
                remote(here, here, new_sem.at[1], gather_left.at[jnp.maximum(z, 1) - 1, j], down).start()

            remote(here, here, new_sem.at[2], gather_core.at[k], partner).start()

        each_weight(j, do)

        @pl.when(j + 2 < steps)
        def _():
            load_state(j + 2)

    def retire(j):
        q = j % RING
        for n in range(last):
            b = last - n

            @pl.when(b > z)
            def _(b=b):
                remote(right.at[b - 1, q], right.at[b - 1, q], right_send.at[b - 1, q], right_recv.at[b - 1, q], up).wait_send()

            @pl.when(n < z)
            def _(n=n):
                remote(left.at[n, q], left.at[n, q], left_send.at[n, q], left_recv.at[n, q], down).wait_send()

        @pl.when((j < steps - RING) & (z > 0))
        def _():
            pl.semaphore_signal(right_free, inc=1, device_id=down, device_id_type=MESH)

        @pl.when((j < steps - RING) & (z < last))
        def _():
            pl.semaphore_signal(left_free, inc=1, device_id=up, device_id_type=MESH)

    def relay(b, j, slot, recv, sent, to, more):
        def do(k, layer, rows, cols):
            here = wo[k].at[layer, b, c, rows, cols]
            remote(here, here, sent.at[slot], recv.at[slot, j], to).wait_recv()

            @pl.when(more)
            def _():
                remote(here, here, sent.at[slot], recv.at[slot, j], to).start()

            remote(here, here, relay_core, gather_core.at[k], partner).start()

        each_weight(j, do)

    done_at = [LAG * max(b, last - b) for b in range(CHIPS)]
    mine = LAG * jnp.maximum(z, last - z)

    for j in range(AHEAD):
        load_terms(j)
    for j in range(2):
        load_state(j)

    def within(j):
        return (j >= 0) & (j < steps)

    @pl.loop(0, steps + 2 * last * LAG)
    def _(i):
        @pl.when(i + AHEAD < steps)
        def _():
            load_terms(i + AHEAD)

        @pl.when(i < steps)
        def _():
            pltpu.make_async_copy(own.at[i % OWN], own.at[i % OWN], own_sem.at[i % OWN]).wait()
            t = i % THEIRS
            remote(theirs.at[t], theirs.at[t], theirs_send, theirs_recv.at[t], partner).wait_recv()

        j_right = i - LAG * z
        j_left = i - LAG * (last - z)
        j_old = i - mine - 1

        @pl.when(within(j_old))
        def _():
            retire(j_old)

        @pl.when((j_right >= RING) & (j_right < steps) & (z < last))
        def _():
            pl.semaphore_wait(right_free, 1)

        @pl.when((j_left >= RING) & (j_left < steps) & (z > 0))
        def _():
            pl.semaphore_wait(left_free, 1)

        for n in range(last):
            b = last - n

            @pl.when(within(j_right) & (b > z))
            def _(b=b):
                forward(right, b - 1, b, j_right, right_send, right_recv, up, z == 0)

            @pl.when(within(j_left) & (n < z))
            def _(n=n):
                forward(left, n, n, j_left, left_send, left_recv, down, z == last)

        j_mine = i - mine

        @pl.when(within(j_mine))
        def _():
            final(j_mine)

        j_free = i - last * LAG

        @pl.when((j_free >= 0) & (j_free < steps - THEIRS))
        def _():
            pl.semaphore_signal(theirs_free, inc=1, device_id=partner, device_id_type=MESH)

        for n in range(last):
            b = last - n
            j = i - done_at[n] - LAG * (z - n)

            @pl.when(within(j) & (n < z))
            def _(n=n, j=j):
                relay(n, j, n, gather_right, relay_right, up, z < last)

            j = i - done_at[b] - LAG * (b - z)

            @pl.when(within(j) & (b > z))
            def _(b=b, j=j):
                relay(b, j, b - 1, gather_left, relay_left, down, z > 0)

    for k in range(3):
        sent = g[k].at[:, :, 1 - c]
        remote(sent, sent, theirs_send, gather_core.at[k], partner).wait_send()
        one = wo[k].at[:, 0, 0]
        for _ in range(last):
            remote(one, one, relay_core, gather_core.at[k], partner).wait_send()
        remote(one, one, new_sem.at[2], gather_core.at[k], partner).wait_send()

        @pl.when(z < last)
        def _():
            remote(one, one, new_sem.at[0], gather_core.at[k], up).wait_send()

        @pl.when(z > 0)
        def _():
            remote(one, one, new_sem.at[1], gather_core.at[k], down).wait_send()

        for n in range(last):
            b = last - n

            @pl.when((n < z) & (z < last))
            def _(n=n):
                remote(one, one, relay_right.at[n], gather_core.at[k], up).wait_send()

            @pl.when((b > z) & (z > 0))
            def _(b=b):
                remote(one, one, relay_left.at[b - 1], gather_core.at[k], down).wait_send()

    for k in range(3):
        arrived = wo[k].at[:, :, 1 - c]
        remote(arrived, arrived, theirs_send, gather_core.at[k], partner).wait_recv()


def finish(steps, *refs):
    w, m, v = refs[:3], refs[3], refs[4]
    wo, mo, vo = (refs[i : i + 3] for i in range(5, 14, 3))
    w_sem, m_sem, v_sem = refs[14:]
    per = steps // 3
    for k in range(3):
        layers, chips, cores, r, _ = w[k].shape

        @pl.loop(0, layers * chips * cores)
        def _(n, k=k, each=chips * cores, cores=cores, r=r):
            layer, b = n // each, n % each
            rows = pl.ds(pl.multiple_of(b * r, r), r)
            pltpu.make_async_copy(w[k].at[layer, b // cores, b % cores], wo[k].at[layer, rows], w_sem.at[k]).start()

        @pl.loop(0, per)
        def _(j, k=k):
            layer, row, col = piece(j, per, mo[k].shape[1], mo[k].shape[2])
            place = (layer, pl.ds(row, ROWS), pl.ds(col, COLS))
            pltpu.make_async_copy(m.at[k * per + j], mo[k].at[place], m_sem).start()
            pltpu.make_async_copy(v.at[k * per + j], vo[k].at[place], v_sem).start()

    for k in range(3):
        pltpu.make_async_copy(w[k], w[k], w_sem.at[k]).wait()
    pltpu.make_async_copy(m, m, m_sem).wait()
    pltpu.make_async_copy(v, v, v_sem).wait()


def solution(mesh):
    cores = mesh.shape["dp"] // CHIPS

    def step(*arrays):
        terms, weights, m, v = (arrays[i : i + 3] for i in (0, 3, 6, 9))
        steps = 3 * m[0].size // (ROWS * COLS)
        split = lambda a, one: a.reshape(one.shape[0], CHIPS, cores, *one.shape[1:])
        g = [split(a, one) for a, one in zip(terms, m, strict=True)]
        w = [split(a, one) for a, one in zip(weights, m, strict=True)]
        any_space, hbm, vmem = (pl.BlockSpec(memory_space=a) for a in (pl.ANY, pltpu.HBM, pltpu.VMEM))
        dma = pltpu.SemaphoreType.DMA
        half, full = jnp.bfloat16, jnp.float32
        state = (steps, ROWS, COLS)
        got = pl.pallas_call(
            functools.partial(kernel, steps),
            out_shape=[*(pltpu.VMEM(a.shape, a.dtype) for a in w), pltpu.VMEM(state, full), pltpu.VMEM(state, full)],
            in_specs=[any_space] * 12,
            out_specs=[vmem] * 5,
            scratch_shapes=[
                pltpu.VMEM((OWN, CHIPS, ROWS, COLS), half),
                pltpu.VMEM((THEIRS, CHIPS, ROWS, COLS), half),
                pltpu.VMEM((CHIPS - 1, RING, ROWS, COLS), half),
                pltpu.VMEM((CHIPS - 1, RING, ROWS, COLS), half),
                pltpu.VMEM((SLOTS, ROWS, COLS), half),
                pltpu.VMEM((SLOTS, ROWS, COLS), full),
                pltpu.VMEM((SLOTS, ROWS, COLS), full),
                dma((OWN,)),
                dma,
                dma((THEIRS,)),
                pltpu.SemaphoreType.REGULAR,
                dma((CHIPS - 1, RING)),
                dma((CHIPS - 1, RING)),
                pltpu.SemaphoreType.REGULAR,
                dma((CHIPS - 1, RING)),
                dma((CHIPS - 1, RING)),
                pltpu.SemaphoreType.REGULAR,
                dma((3, SLOTS)),
                dma((3,)),
                dma((CHIPS - 1,)),
                dma((CHIPS - 1,)),
                dma,
                dma((CHIPS - 1, steps)),
                dma((CHIPS - 1, steps)),
                dma((3,)),
            ],
            compiler_params=pltpu.CompilerParams(collective_id=0, has_side_effects=True, vmem_limit_bytes=GRANT),
            name="sum_step_gather",
        )(*g, *w, *m, *v)
        held = [pltpu.with_memory_space_constraint(a, pltpu.VMEM) for a in got]
        return pl.pallas_call(
            functools.partial(finish, steps),
            out_shape=[pltpu.HBM(a.shape, a.dtype) for a in (*weights, *m, *v)],
            in_specs=[vmem] * 5,
            out_specs=[hbm] * 9,
            scratch_shapes=[dma((3,)), dma, dma],
            compiler_params=pltpu.CompilerParams(vmem_limit_bytes=GRANT),
            name="finish",
        )(*held)

    all_of, cut = P(None, None, None), P(None, "dp", None)
    return jax.shard_map(
        step,
        mesh=mesh,
        in_specs=(P(("rep", "dp"), None, None, None),) * 3 + (all_of,) * 3 + (cut,) * 6,
        out_specs=(P("rep", None, None),) * 3 + (P("rep", "dp", None),) * 6,
        check_vma=False,
    )
```

time: 464 us -> 447 us (0.963)
  Pallas kernels: 463 us -> 447 us
    pallas_call x1, Pallas kernels: 31.3 us -> 17.8 us  [step(): pl.pallas_call(functools.partial(finish, steps), out_shape=[pltpu.HBM(a.s...]
where the time goes in v3:
time: 447 us
  Pallas kernels  447 us (100%)
    pallas_call x1, Pallas kernels, step(): pl.pallas_call(functools.partial(kernel, steps), out_shape=[*(pltpu.VMEM(...  429 us
    pallas_call x1, Pallas kernels, step(): pl.pallas_call(functools.partial(finish, steps), out_shape=[pltpu.HBM(a.s...  17.8 us

profile of v3, /device:TPU:0, one launch (start us, length us, event | category | flops | bytes accessed | tf_op | source)
XLA Modules:
  0.0 447.3 jit_solution(17287945944986690085)
XLA Ops:
  0.6 428.9 %sum_step_gather.1 = (bf16[2,4,2,128,3072]{4,3,2,1,0:T(8,128)(2,1)S(1)}, bf16[2,4,2,128,3072]{4,3,2,1,0:T(8,128)(2,1)S(1)}, bf16[2,4,2,384,1024]{4,3,2,1,0:T(8,1...) custom-call(bf16[2,4,2,128,3072]{4,3,2,1,0:T(8,128)(2,1)} %bitcast.6, bf16[2,4,2,128,3072]{4,3,2,1,0:T(8,128)(2,1)} %bitcast.7, ...), custom_call_target="tpu_custom_call" | custom-call | tf_op jit(solution)/shard_map/sum_step_gather/pallas_call | solution.py:367
  429.6 17.8 %finish.1 = (bf16[2,1024,3072]{2,1,0:T(8,128)(2,1)}, bf16[2,1024,3072]{2,1,0:T(8,128)(2,1)}, bf16[2,3072,1024]{2,1,0:T(8,128)(2,1)}, f32[2,128,3072]{2,1,0:T(8,1...) custom-call(bf16[2,4,2,128,3072]{4,3,2,1,0:T(8,128)(2,1)S(1)} %get-t, ...), custom_call_target="tpu_custom_call" | custom-call | tf_op jit(solution)/shard_map/finish/pallas_call | solution.py:403

commit v4 on v3

--- a/solution.py
+++ b/solution.py
@@ -16,7 +16,8 @@
 OWN = AHEAD + 3 * LAG + 1
 SLOTS = 4
 THEIRS = OWN + 2
-RING = 8
+GATHER = 8
+RING = 6
 GRANT = 9_400_000
 BAND = 16
 
@@ -168,11 +169,11 @@
 
             @pl.when(z < last)
             def _():
-                remote(here, here, new_sem.at[0], gather_right.at[jnp.minimum(z, 2), j], up).start()
+                remote(here, here, new_sem.at[0], gather_right.at[jnp.minimum(z, 2), j % GATHER], up).start()
 
             @pl.when(z > 0)
             def _():
-                remote(here, here, new_sem.at[1], gather_left.at[jnp.maximum(z, 1) - 1, j], down).start()
+                remote(here, here, new_sem.at[1], gather_left.at[jnp.maximum(z, 1) - 1, j % GATHER], down).start()
 
             remote(here, here, new_sem.at[2], gather_core.at[k], partner).start()
 
@@ -206,11 +207,11 @@
     def relay(b, j, slot, recv, sent, to, more):
         def do(k, layer, rows, cols):
             here = wo[k].at[layer, b, c, rows, cols]
-            remote(here, here, sent.at[slot], recv.at[slot, j], to).wait_recv()
+            remote(here, here, sent.at[slot], recv.at[slot, j % GATHER], to).wait_recv()
 
             @pl.when(more)
             def _():
-                remote(here, here, sent.at[slot], recv.at[slot, j], to).start()
+                remote(here, here, sent.at[slot], recv.at[slot, j % GATHER], to).start()
 
             remote(here, here, relay_core, gather_core.at[k], partner).start()
 
@@ -392,8 +393,8 @@
                 dma((CHIPS - 1,)),
                 dma((CHIPS - 1,)),
                 dma,
-                dma((CHIPS - 1, steps)),
-                dma((CHIPS - 1, steps)),
+                dma((CHIPS - 1, GATHER)),
+                dma((CHIPS - 1, GATHER)),
                 dma((3,)),
             ],
             compiler_params=pltpu.CompilerParams(collective_id=0, has_side_effects=True, vmem_limit_bytes=GRANT),

time: 447 us -> 444 us (level)
  no operation moved by 1% of the time
where the time goes in v4:
time: 444 us
  Pallas kernels  443 us (100%)
    pallas_call x1, Pallas kernels, step(): pl.pallas_call(functools.partial(kernel, steps), out_shape=[*(pltpu.VMEM(...  425 us
    pallas_call x1, Pallas kernels, step(): pl.pallas_call(functools.partial(finish, steps), out_shape=[pltpu.HBM(a.s...  17.8 us

profile of v4, /device:TPU:0, one launch (start us, length us, event | category | flops | bytes accessed | tf_op | source)
XLA Modules:
  0.0 443.7 jit_solution(12532552857556932086)
XLA Ops:
  0.6 425.3 %sum_step_gather.1 = (bf16[2,4,2,128,3072]{4,3,2,1,0:T(8,128)(2,1)S(1)}, bf16[2,4,2,128,3072]{4,3,2,1,0:T(8,128)(2,1)S(1)}, bf16[2,4,2,384,1024]{4,3,2,1,0:T(8,1...) custom-call(bf16[2,4,2,128,3072]{4,3,2,1,0:T(8,128)(2,1)} %bitcast.6, bf16[2,4,2,128,3072]{4,3,2,1,0:T(8,128)(2,1)} %bitcast.7, ...), custom_call_target="tpu_custom_call" | custom-call | tf_op jit(solution)/shard_map/sum_step_gather/pallas_call | solution.py:368
  425.9 17.8 %finish.1 = (bf16[2,1024,3072]{2,1,0:T(8,128)(2,1)}, bf16[2,1024,3072]{2,1,0:T(8,128)(2,1)}, bf16[2,3072,1024]{2,1,0:T(8,128)(2,1)}, f32[2,128,3072]{2,1,0:T(8,1...) custom-call(bf16[2,4,2,128,3072]{4,3,2,1,0:T(8,128)(2,1)S(1)} %get-t, ...), custom_call_target="tpu_custom_call" | custom-call | tf_op jit(solution)/shard_map/finish/pallas_call | solution.py:404

commit v5 on v4

--- a/solution.py
+++ b/solution.py
@@ -14,10 +14,10 @@
 LAG = 1
 AHEAD = 2
 OWN = AHEAD + 3 * LAG + 1
-SLOTS = 4
-THEIRS = OWN + 2
-GATHER = 8
-RING = 6
+SLOTS = 3
+THEIRS = OWN + 1
+GATHER = 6
+RING = 5
 GRANT = 9_400_000
 BAND = 16
 

time: 444 us -> 444 us (level)
  no operation moved by 1% of the time
where the time goes in v5:
time: 444 us; the launch traced here: 443 us
  Pallas kernels  443 us (100%)
    pallas_call x1, Pallas kernels, step(): pl.pallas_call(functools.partial(kernel, steps), out_shape=[*(pltpu.VMEM(...  425 us
    pallas_call x1, Pallas kernels, step(): pl.pallas_call(functools.partial(finish, steps), out_shape=[pltpu.HBM(a.s...  17.8 us

profile of v5, /device:TPU:0, one launch (start us, length us, event | category | flops | bytes accessed | tf_op | source)
XLA Modules:
  0.0 443.4 jit_solution(7165959019599400502)
XLA Ops:
  0.6 425.0 %sum_step_gather.1 = (bf16[2,4,2,128,3072]{4,3,2,1,0:T(8,128)(2,1)S(1)}, bf16[2,4,2,128,3072]{4,3,2,1,0:T(8,128)(2,1)S(1)}, bf16[2,4,2,384,1024]{4,3,2,1,0:T(8,1...) custom-call(bf16[2,4,2,128,3072]{4,3,2,1,0:T(8,128)(2,1)} %bitcast.6, bf16[2,4,2,128,3072]{4,3,2,1,0:T(8,128)(2,1)} %bitcast.7, ...), custom_call_target="tpu_custom_call" | custom-call | tf_op jit(solution)/shard_map/sum_step_gather/pallas_call | solution.py:368
  425.7 17.8 %finish.1 = (bf16[2,1024,3072]{2,1,0:T(8,128)(2,1)}, bf16[2,1024,3072]{2,1,0:T(8,128)(2,1)}, bf16[2,3072,1024]{2,1,0:T(8,128)(2,1)}, f32[2,128,3072]{2,1,0:T(8,1...) custom-call(bf16[2,4,2,128,3072]{4,3,2,1,0:T(8,128)(2,1)S(1)} %get-t, ...), custom_call_target="tpu_custom_call" | custom-call | tf_op jit(solution)/shard_map/finish/pallas_call | solution.py:404
